TPU v7x, 32 devices: a whole 2x2x4 slice. The times are simulated.
32 devices in a mesh: gx: 16 (over z, y, core), gy: 2 (over x).
Axes of the slice: x: 2, y: 2, z: 4, core: 2. Of those that a mesh axis runs over, the one named last changes fastest.
Arguments:
- old_block: float32 [12288, 24576], P('gx', 'gy'), may hold values from -6 to 6
- vectors: bfloat16 [256, 2, 12288], P(None, 'gy', 'gx'), may hold values from -4 to 4
- prior: bfloat16 [32768, 3072], P('gx', 'gy'), may hold values from -2 to 2
- pair_columns: float32 [32768, 128], P(('gx', 'gy')), may hold values from -6 to 6
- pivots: int32 [128], replicated, may hold values from 0 to 32767
Outputs:
- new_block: float32 [12288, 24576], P('gx', 'gy')
- residual_columns: float32 [32768, 128], P(('gx', 'gy'))
Inputs may be any that keep to these rules, and one draw needn't show every extreme that they name: `pivots`: pivot AO-pair row indices, repeats possible.
All inputs are finite; a program needn't handle non-finite values.
Results may differ from a plain program's by a relative error of at most 0.0055.
Values may be sent and summed in bfloat16 or wider, within the bound.
No kernel may reach another device: no remote copies, remote signals or barrier semaphores. Data moves between devices by JAX's collectives and lax.ppermute only.
A program may use at most 192 MiB of HBM per device.

v0:
```python
import jax
import jax.numpy as jnp
from jax import lax
from jax.sharding import PartitionSpec as P


def from_root(value, axis, root):
    mine = lax.axis_index(axis) == root
    return lax.psum(jnp.where(mine, value, jnp.zeros_like(value)), axis)


def local(old_block, vectors, prior, pair_columns, pivots):
    local_vectors = vectors.reshape(vectors.shape[0], vectors.shape[2])
    slab_part = from_root(local_vectors, "gy", 0)
    gained = jnp.dot(
        slab_part.T,
        lax.all_gather(local_vectors, "gx", axis=1, tiled=True),
        preferred_element_type=jnp.float32,
    )
    new_block = old_block + gained
    rows_local = prior.shape[0]
    offset = lax.axis_index("gx") * rows_local
    local_index = pivots - offset
    inside = jnp.logical_and(local_index >= 0, local_index < rows_local)
    chosen = jnp.take(prior, jnp.clip(local_index, 0, rows_local - 1), axis=0).astype(jnp.float32)
    chosen = chosen * inside[:, None].astype(jnp.float32)
    pivot_block = lax.psum(chosen.astype(jnp.bfloat16), "gx")
    groups = lax.axis_size("gy")
    width = prior.shape[1]
    regrouped = lax.all_to_all(prior, "gy", split_axis=0, concat_axis=1, tiled=True)
    full_pivots = lax.all_gather(pivot_block, "gy", axis=1, tiled=True)
    parts = jnp.einsum(
        "rgc,kgc->grk",
        regrouped.reshape(regrouped.shape[0], groups, width),
        full_pivots.reshape(full_pivots.shape[0], groups, width),
        preferred_element_type=jnp.float32,
    )
    rounded = lax.optimization_barrier(parts.astype(jnp.bfloat16))
    intersection = jnp.sum(rounded.astype(jnp.float32), axis=0)
    return (new_block, pair_columns - intersection)


def solution(mesh):
    placed = (P("gx", "gy"), P(None, "gy", "gx"), P("gx", "gy"), P(("gx", "gy"), None), P())
    return jax.shard_map(
        local,
        mesh=mesh,
        in_specs=placed,
        out_specs=(P("gx", "gy"), P(("gx", "gy"), None)),
        check_vma=False,
    )
```

profile of v0, /device:TPU:0, one launch (start us, length us, event | category | flops | bytes accessed | tf_op | source)
XLA Modules:
  0.0 236.3 jit_solution(9439408910341760958)
XLA Ops:
  7.2 0.0 all-reduce.5.cloned.1.call-start
  7.2 0.7 compare_and_fusion
  7.9 4.8 %gather_fusion = bf16[128,1536]{1,0:T(8,128)(2,1)S(1)} fusion(bf16[2048,1536]{1,0:T(8,128)(2,1)} %param.7, s32[1024]{0:T(1024)S(1)} %pad_clamp_fusion), kind=kCustom, calls=%fused_computation | custom fusion | bytes 786944 | tf_op jit(solution)/shard_map/jit(_take)/gather | solution.py:25
  12.7 0.9 multiply_convert_fusion
  13.7 0.0 all-reduce.5.cloned.1.call-update
  13.7 0.0 all-reduce.3.cloned.1.call-start
  13.8 1.8 select_bitcast_fusion
  15.6 0.0 all-reduce.3.cloned.1.call-update
  15.6 0.0 all-gather.3.cloned.1.call-start
  15.6 0.7 all-gather.3.cloned.1.call-update
  16.3 0.0 copy-start
  16.3 6.5 %all-to-all-start = ((bf16[2,1024,1536]{2,1,0:T(8,128)(2,1)}), bf16[2,1024,1536]{2,1,0:T(8,128)(2,1)}, u32[]{:S(2)}, u32[]{:S(2)}) async-start(bf16[2,1024,1536]{2,1,0:T(8,128)(2,1)} %bitcast.18), calls=%async_computation | async-start | bytes 12582912 | tf_op jit(solution)/shard_map/all_to_all | solution.py:30
  22.8 0.0 copy-done
  22.8 0.2 copy.11
  23.0 84.9 %all-reduce.5.cloned.1.call-done = bf16[128,1536]{1,0:T(8,128)(2,1)} async-done(((bf16[128,1536]{1,0:T(8,128)(2,1)}), bf16[128,1536]{1,0:T(8,128)(2,1)}) %all-reduce.5.cloned.1.call-update) | async-done | bytes 393232 | tf_op jit(solution)/shard_map/psum | solution.py:27
  107.9 14.1 %all_gather.7 = bf16[128,3072]{1,0:T(8,128)(2,1)S(1)} all-gather(bf16[128,1536]{1,0:T(8,128)(2,1)} %all-reduce.5.cloned.1.call-done), channel_id=1, replica_groups=mesh['gx'=16,'gy'=2] {'gy'}, dimensions={1}, use_global_device_ids=true | all-gather | bytes 1179648 | tf_op jit(solution)/shard_map/all_gather | solution.py:31
  122.1 0.4 copy.9
  122.4 0.0 all-to-all-done
  122.4 5.0 %fusion.6 = bf16[2,1024,128]{1,2,0:T(8,128)(2,1)S(1)} fusion(bf16[128,2,1536]{0,2,1:T(8,128)(2,1)S(1)} %bitcast.19, bf16[2,1024,1536]{2,1,0:T(8,128)(2,1)} %all-to-all-done), kind=kOutput, calls=%fused_computation.6 | convolution fusion | flops 805568512 | bytes 7602176 | tf_op jit(solution)/shard_map/rgc,kgc->grk/dot_general | solution.py:32
  127.5 0.1 convert_reduce_fusion
  127.6 0.1 sub.11
  127.6 1.0 copy.12
  128.6 7.6 %all-reduce.3.cloned.1.call-done = bf16[256,768]{1,0:T(8,128)(2,1)} async-done(((bf16[256,768]{1,0:T(8,128)(2,1)}), bf16[256,768]{1,0:T(8,128)(2,1)}) %all-reduce.3.cloned.1.call-update) | async-done | bytes 393232 | tf_op jit(solution)/shard_map/psum | solution.py:9
  136.2 63.9 %all-gather.3.cloned.1.call-done = bf16[256,1,12288]{2,0,1:T(8,128)(2,1)} async-done(((bf16[256,1,768]{2,0,1:T(8,128)(2,1)}), bf16[256,1,12288]{2,0,1:T(8,128)(2,1)}) %all-gather.3.cloned.1.call-update) | async-done | bytes 6291472 | tf_op jit(solution)/shard_map/all_gather | solution.py:17
  200.1 29.6 %convolution_add_fusion = f32[768,12288]{1,0:T(8,128)} fusion(f32[768,12288]{1,0:T(8,128)} %param.5, bf16[256,768]{1,0:T(8,128)(2,1)} %all-reduce.3.cloned.1.call-done, bf16[256,1,12288]{2,0,1:T(8,128)(2,1)} %all-gather.3.cloned.1.call-done), kind=kOutput, calls=%fused_computation.1 | convolution fusion | flops 4841275392 | bytes 82182144 | tf_op jit(solution)/shard_map/dot_general | solution.py:15
  (1 shorter events, 0.0 us)
Async XLA Ops:
  7.2 100.7 %all-reduce.5.cloned.1.call-start = ((), (), s32[]{:S(2)}) async-start(), calls=%async_computation.2 | async-start | bytes 786432 | tf_op jit(solution)/shard_map/psum | solution.py:27
  13.7 122.5 %all-reduce.3.cloned.1.call-start = ((), (), s32[]{:S(2)}) async-start(), calls=%async_computation.1 | async-start | bytes 786432 | tf_op jit(solution)/shard_map/psum | solution.py:9
  15.6 184.5 %all-gather.3.cloned.1.call-start = ((), (), s32[]{:S(2)}) async-start(), calls=%async_computation.3 | async-start | bytes 6684672 | tf_op jit(solution)/shard_map/all_gather | solution.py:17
  16.3 6.5 %copy-start = (f32[1024,128]{1,0:T(8,128)S(1)}, f32[1024,128]{1,0:T(8,128)}, u32[]{:S(2)}) copy-start(f32[1024,128]{1,0:T(8,128)} %param.8) | copy-start | bytes 1572868
  16.3 106.1 %all-to-all-start = ((bf16[2,1024,1536]{2,1,0:T(8,128)(2,1)}), bf16[2,1024,1536]{2,1,0:T(8,128)(2,1)}, u32[]{:S(2)}, u32[]{:S(2)}) async-start(bf16[2,1024,1536]{2,1,0:T(8,128)(2,1)} %bitcast.18), calls=%async_computation | async-start | bytes 12582912 | tf_op jit(solution)/shard_map/all_to_all | solution.py:30
Sparse Core Ops, SparseCore 0:
  13.8 94.0 all-reduce.4
  110.8 25.4 all-reduce.2
  138.5 61.5 all-gather.2
where the time goes:
time: 237 us; the launch traced here: 236 us
  waiting for transfers between devices  157 us (66%)
  matrix products  34.7 us (15%)
  blocking collectives  14.1 us (6%)
  between operations  13.8 us (6%)
  starting transfers between devices  6.59 us (3%)
  local copies, waits for them, and re-layouts  6.42 us (3%)
  other arithmetic  3.57 us (2%)
    psum x1, waiting for transfers between devices, local(): pivot_block = lax.psum(chosen.astype(jnp.bfloat16), 'gx')  84.9 us
    all_gather x1, waiting for transfers between devices, local(): lax.all_gather(local_vectors, 'gx', axis=1, tiled=True)  63.9 us
    dot_general x1, matrix products, local(): jnp.dot(slab_part.T, lax.all_gather(local_vectors, 'gx', axis=1, tiled=Tr...  29.6 us
    all_gather x1, blocking collectives, local(): full_pivots = lax.all_gather(pivot_block, 'gy', axis=1, tiled=True)  14.1 us
    psum x1, waiting for transfers between devices, from_root(): return lax.psum(jnp.where(mine, value, jnp.zeros_like(value)), axis)  7.58 us
    all_to_all x1, starting transfers between devices, local(): lax.all_to_all(prior, 'gy', split_axis=0, concat_axis=1, tiled=True)  6.47 us
    dot_general x1, matrix products, local(): jnp.einsum('rgc,kgc->grk', regrouped.reshape(regrouped.shape[0], groups,...  5.02 us
    gather x1, local copies, waits for them, and re-layouts, local(): jnp.take(prior, jnp.clip(local_index, 0, rows_local - 1), axis=0)  4.85 us
  transfers between devices with their start and end apart: 4, of which 3 were waited for; matrix products, arithmetic and copies ran while one was open for 4% of the time, Pallas kernels for 0%

commit v1 on v0

--- a/solution.py
+++ b/solution.py
@@ -24,7 +24,7 @@
     inside = jnp.logical_and(local_index >= 0, local_index < rows_local)
     chosen = jnp.take(prior, jnp.clip(local_index, 0, rows_local - 1), axis=0).astype(jnp.float32)
     chosen = chosen * inside[:, None].astype(jnp.float32)
-    pivot_block = lax.psum(chosen.astype(jnp.bfloat16), "gx")
+    pivot_block = jnp.sum(lax.all_gather(chosen.astype(jnp.bfloat16), "gx"), axis=0)
     groups = lax.axis_size("gy")
     width = prior.shape[1]
     regrouped = lax.all_to_all(prior, "gy", split_axis=0, concat_axis=1, tiled=True)

time: 237 us -> 179 us (0.76)
  waiting for transfers between devices: 157 us -> 79.5 us
  blocking collectives: 14.1 us -> 28.5 us
  other arithmetic: 3.57 us -> 7.35 us
    psum x1 -> x0, waiting for transfers between devices: 84.9 us -> none  [local(): pivot_block = lax.psum(chosen.astype(jnp.bfloat16), 'gx')]
    all_gather x0 -> x1, waiting for transfers between devices: none -> 55 us  [local(): lax.all_gather(chosen.astype(jnp.bfloat16), 'gx')]
    all_gather x1, waiting for transfers between devices: 63.9 us -> 23.7 us  [local(): lax.all_gather(local_vectors, 'gx', axis=1, tiled=True)]
    all_gather x1, blocking collectives: 14.1 us -> 28.5 us  [local(): full_pivots = lax.all_gather(pivot_block, 'gy', axis=1, tiled=True)]
    psum x1, waiting for transfers between devices: 7.58 us -> 0.01 us  [from_root(): return lax.psum(jnp.where(mine, value, jnp.zeros_like(value)), axis)]
    reduce_sum x0 -> x1, other arithmetic: none -> 3.78 us  [local(): jnp.sum(lax.all_gather(chosen.astype(jnp.bfloat16), 'gx'), axis=0)]
  transfers between devices with their start and end apart: 4 -> 4, of which waited for: 3 -> 2; matrix products, arithmetic and copies ran while one was open for 4% -> 7% of each run, Pallas kernels for 0% -> 0%
where the time goes in v1:
time: 179 us; the launch traced here: 178 us
  waiting for transfers between devices  79.5 us (44%)
  matrix products  34.6 us (19%)
  blocking collectives  28.5 us (16%)
  between operations  15.6 us (9%)
  other arithmetic  7.35 us (4%)
  starting transfers between devices  6.54 us (4%)
  local copies, waits for them, and re-layouts  6.42 us (4%)
    all_gather x1, waiting for transfers between devices, local(): lax.all_gather(chosen.astype(jnp.bfloat16), 'gx')  55 us
    dot_general x1, matrix products, local(): jnp.dot(slab_part.T, lax.all_gather(local_vectors, 'gx', axis=1, tiled=Tr...  29.6 us
    all_gather x1, blocking collectives, local(): full_pivots = lax.all_gather(pivot_block, 'gy', axis=1, tiled=True)  28.5 us
    all_gather x1, waiting for transfers between devices, local(): lax.all_gather(local_vectors, 'gx', axis=1, tiled=True)  23.7 us
    all_to_all x1, starting transfers between devices, local(): lax.all_to_all(prior, 'gy', split_axis=0, concat_axis=1, tiled=True)  6.41 us
    dot_general x1, matrix products, local(): jnp.einsum('rgc,kgc->grk', regrouped.reshape(regrouped.shape[0], groups,...  4.98 us
    gather x1, local copies, waits for them, and re-layouts, local(): jnp.take(prior, jnp.clip(local_index, 0, rows_local - 1), axis=0)  4.85 us
    reduce_sum x1, other arithmetic, local(): jnp.sum(lax.all_gather(chosen.astype(jnp.bfloat16), 'gx'), axis=0)  3.78 us
  transfers between devices with their start and end apart: 4, of which 2 were waited for; matrix products, arithmetic and copies ran while one was open for 7% of the time, Pallas kernels for 0%

profile of v1, /device:TPU:0, one launch (start us, length us, event | category | flops | bytes accessed | tf_op | source)
XLA Modules:
  0.0 178.5 jit_solution(13651474671282826932)
XLA Ops:
  8.0 0.0 all-gather.4.cloned.1.call-start
  8.0 0.7 compare_and_fusion
  8.7 4.8 %gather_fusion = bf16[128,1536]{1,0:T(8,128)(2,1)S(1)} fusion(bf16[2048,1536]{1,0:T(8,128)(2,1)} %param.7, s32[1024]{0:T(1024)S(1)} %pad_clamp_fusion), kind=kCustom, calls=%fused_computation | custom fusion | bytes 786944 | tf_op jit(solution)/shard_map/jit(_take)/gather | solution.py:25
  13.6 0.9 multiply_convert_fusion
  14.5 0.0 all-gather.4.cloned.1.call-update
  14.6 0.0 all-reduce.2.cloned.1.call-start
  14.6 1.8 select_bitcast_fusion
  16.4 0.0 all-reduce.2.cloned.1.call-update
  16.4 0.0 all-gather.6.cloned.1.call-start
  16.5 0.7 all-gather.6.cloned.1.call-update
  17.2 0.0 copy-start
  17.2 6.4 %all-to-all-start = ((bf16[2,1024,1536]{2,1,0:T(8,128)(2,1)}), bf16[2,1024,1536]{2,1,0:T(8,128)(2,1)}, u32[]{:S(2)}, u32[]{:S(2)}) async-start(bf16[2,1024,1536]{2,1,0:T(8,128)(2,1)} %bitcast.22), calls=%async_computation | async-start | bytes 12582912 | tf_op jit(solution)/shard_map/all_to_all | solution.py:30
  23.6 0.0 copy-done
  23.6 0.2 copy.10
  23.8 55.0 %all-gather.4.cloned.1.call-done = bf16[16,128,1536]{2,1,0:T(8,128)(2,1)} async-done(((bf16[1,128,1536]{2,1,0:T(8,128)(2,1)}), bf16[16,128,1536]{2,1,0:T(8,128)(2,1)}) %all-gather.4.cloned.1.call-update) | async-done | bytes 6291472 | tf_op jit(solution)/shard_map/all_gather | solution.py:27
  78.8 3.8 %reduce_sum.21 = bf16[128,1536]{1,0:T(8,128)(2,1)S(1)} reduce(bf16[16,128,1536]{2,1,0:T(8,128)(2,1)} %all-gather.4.cloned.1.call-done, bf16[]{:T(256)} %constant.12.clone.1), dimensions={0}, to_apply=%region_1.2 | reduce | flops 2949120 | bytes 6684674 | tf_op jit(solution)/shard_map/reduce_sum | solution.py:27
  82.6 28.5 %all_gather.12 = bf16[128,3072]{1,0:T(8,128)(2,1)S(1)} all-gather(bf16[128,1536]{1,0:T(8,128)(2,1)S(1)} %reduce_sum.21), channel_id=1, replica_groups=mesh['gx'=16,'gy'=2] {'gy'}, dimensions={1}, use_global_device_ids=true | all-gather | bytes 1179648 | tf_op jit(solution)/shard_map/all_gather | solution.py:31
  111.1 0.4 copy.8
  111.5 0.0 all-to-all-done
  111.5 5.0 %fusion.6 = bf16[2,1024,128]{1,2,0:T(8,128)(2,1)S(1)} fusion(bf16[128,2,1536]{0,2,1:T(8,128)(2,1)S(1)} %bitcast.23, bf16[2,1024,1536]{2,1,0:T(8,128)(2,1)} %all-to-all-done), kind=kOutput, calls=%fused_computation.6 | convolution fusion | flops 805568512 | bytes 7602176 | tf_op jit(solution)/shard_map/rgc,kgc->grk/dot_general | solution.py:32
  116.5 0.1 convert_reduce_fusion
  116.6 0.1 sub.11
  116.7 1.0 copy.11
  117.7 0.0 all-reduce.2.cloned.1.call-done
  117.7 23.7 %all-gather.6.cloned.1.call-done = bf16[256,1,12288]{2,0,1:T(8,128)(2,1)} async-done(((bf16[256,1,768]{2,0,1:T(8,128)(2,1)}), bf16[256,1,12288]{2,0,1:T(8,128)(2,1)}) %all-gather.6.cloned.1.call-update) | async-done | bytes 6291472 | tf_op jit(solution)/shard_map/all_gather | solution.py:17
  141.4 29.6 %convolution_add_fusion = f32[768,12288]{1,0:T(8,128)} fusion(f32[768,12288]{1,0:T(8,128)} %param.5, bf16[256,768]{1,0:T(8,128)(2,1)} %all-reduce.2.cloned.1.call-done, bf16[256,1,12288]{2,0,1:T(8,128)(2,1)} %all-gather.6.cloned.1.call-done), kind=kOutput, calls=%fused_computation.1 | convolution fusion | flops 4841275392 | bytes 82182144 | tf_op jit(solution)/shard_map/dot_general | solution.py:15
  (1 shorter events, 0.0 us)
Async XLA Ops:
  8.0 70.8 %all-gather.4.cloned.1.call-start = ((), (), s32[]{:S(2)}) async-start(), calls=%async_computation.2 | async-start | bytes 6684672 | tf_op jit(solution)/shard_map/all_gather | solution.py:27
  14.6 103.1 %all-reduce.2.cloned.1.call-start = ((), (), s32[]{:S(2)}) async-start(), calls=%async_computation.1 | async-start | bytes 786432 | tf_op jit(solution)/shard_map/psum | solution.py:9
  16.4 125.0 %all-gather.6.cloned.1.call-start = ((), (), s32[]{:S(2)}) async-start(), calls=%async_computation.3 | async-start | bytes 6684672 | tf_op jit(solution)/shard_map/all_gather | solution.py:17
  17.2 6.4 %copy-start = (f32[1024,128]{1,0:T(8,128)S(1)}, f32[1024,128]{1,0:T(8,128)}, u32[]{:S(2)}) copy-start(f32[1024,128]{1,0:T(8,128)} %param.8) | copy-start | bytes 1572868
  17.2 94.3 %all-to-all-start = ((bf16[2,1024,1536]{2,1,0:T(8,128)(2,1)}), bf16[2,1024,1536]{2,1,0:T(8,128)(2,1)}, u32[]{:S(2)}, u32[]{:S(2)}) async-start(bf16[2,1024,1536]{2,1,0:T(8,128)(2,1)} %bitcast.22), calls=%async_computation | async-start | bytes 12582912 | tf_op jit(solution)/shard_map/all_to_all | solution.py:30
Sparse Core Ops, SparseCore 0:
  14.7 64.1 all-gather.3
  81.1 60.2 all-gather.5
Sparse Core Ops, SparseCore 1:
  17.9 37.0 all-reduce.1
